TPU v7x, 32 devices: a whole 2x2x4 slice. The times are simulated.
32 devices in a mesh: seq: 16 (over z, x, core), tp: 2 (over y).
Axes of the slice: x: 2, y: 2, z: 4, core: 2. Of those that a mesh axis runs over, the one named last changes fastest.
Arguments:
- hidden_in: bfloat16 [2048, 4096], P('seq', 'tp'), may hold values from -64 to 64
- span_order: int32 [16], replicated, may hold values from 0 to 15, each once
- norm_gain: bfloat16 [4096], P('tp'), may hold values from 0.099609375 to 1.8984375
- w_query: bfloat16 [4096, 4096], P('seq', 'tp'), may hold values from -0.09375 to 0.09375
- bias_query: bfloat16 [4096], P('tp'), may hold values from -14 to 14
- key_value_weight: bfloat16 [4096, 2, 1024], P('seq', None, 'tp'), may hold values from -0.09375 to 0.09375
- bias_kv: bfloat16 [2, 1024], P(None, 'tp'), may hold values from -14 to 14
- w_out: bfloat16 [4096, 4096], P('tp', 'seq'), may hold values from -0.09375 to 0.09375
- post_gain: bfloat16 [4096], P('tp'), may hold values from 0.099609375 to 1.8984375
Outputs:
- attn_out: bfloat16 [2048, 4096], P('seq', 'tp')
- normed: bfloat16 [2048, 4096], P('seq', 'tp')
Inputs may be any that keep to these rules, and one draw needn't show every extreme that they name: Each span number appears once; row r of hidden_in belongs to span span_order[r // 128].
All inputs are finite; a program needn't handle non-finite values.
Results may differ from a plain program's by a relative error of at most 0.014.
Values may be sent and summed in bfloat16 or wider, within the bound.
A program may use at most 128 MiB of HBM per device.

v0:
```python
import math
import jax
import jax.numpy as jnp
from jax import lax
from jax.sharding import PartitionSpec as P

MODEL_WIDTH = 4096
HEAD_SIZE = 128
GROUP = 4
eps = 1e-06
rope_base = 1000000.0


def apply_rotary(field, token_positions):
    half = field.shape[-1] // 2
    inverse = jnp.exp(-math.log(rope_base) * jnp.arange(half, dtype=jnp.float32) / half)
    angles = token_positions.astype(jnp.float32)[:, None] * inverse[None, :]
    cosine = jnp.cos(angles)[:, None, :]
    sine = jnp.sin(angles)[:, None, :]
    first = field[..., :half]
    second = field[..., half:]
    return jnp.concatenate(
        [first * cosine - second * sine, second * cosine + first * sine], axis=-1
    )


def span_lookup(order, devices):
    table_ids = jnp.arange(order.shape[0], dtype=jnp.int32)
    return jnp.sum(jnp.where(devices[:, None] == table_ids[None, :], order[None, :], 0), axis=1)


def per_device(
    hidden_in,
    span_order,
    norm_gain,
    w_query,
    bias_query,
    key_value_weight,
    bias_kv,
    w_out,
    post_gain,
):
    tok_rows = hidden_in.shape[0]
    seq_index = lax.axis_index("seq")
    own_span = span_lookup(span_order, jnp.full((1,), seq_index, jnp.int32))[0]
    token_positions = own_span * tok_rows + jnp.arange(tok_rows, dtype=jnp.int32)
    local = hidden_in.astype(jnp.float32)
    raw_rows, gains = (
        lax.all_gather(hidden_in, "tp", axis=1, tiled=True),
        lax.all_gather(norm_gain[None, :], "tp", axis=1, tiled=True),
    )
    full_rows = raw_rows.astype(jnp.float32)
    meansq = jnp.mean(full_rows * full_rows, axis=1, keepdims=True)
    normed_in = (full_rows * lax.rsqrt(meansq + eps) * gains.astype(jnp.float32)).astype(
        jnp.bfloat16
    )
    columns = normed_in
    query_proj = jnp.dot(
        columns,
        lax.all_gather(w_query, "seq", axis=0, tiled=True),
        preferred_element_type=jnp.float32,
    )
    columns = normed_in
    pair_proj = jnp.einsum(
        "tr,rkc->tkc",
        columns,
        lax.all_gather(key_value_weight, "seq", axis=0, tiled=True),
        preferred_element_type=jnp.float32,
    )
    query_heads = w_query.shape[1] // HEAD_SIZE
    kv_heads = key_value_weight.shape[2] // HEAD_SIZE
    query_proj = query_proj + bias_query.astype(jnp.float32)[None, :]
    queries = apply_rotary(
        query_proj.reshape(tok_rows, query_heads, HEAD_SIZE), token_positions
    ).astype(jnp.bfloat16)
    pair_proj = pair_proj + bias_kv.astype(jnp.float32)[None, :, :]
    rotated_keys = apply_rotary(
        pair_proj[:, 0, :].reshape(tok_rows, kv_heads, HEAD_SIZE), token_positions
    )
    rotated_keys = rotated_keys.astype(jnp.bfloat16).reshape(tok_rows, kv_heads * HEAD_SIZE)
    value_rows = pair_proj[:, 1, :].astype(jnp.bfloat16)
    grouped = (
        queries.reshape(tok_rows, kv_heads, GROUP, HEAD_SIZE)
        .transpose(1, 2, 0, 3)
        .reshape(kv_heads, GROUP * tok_rows, HEAD_SIZE)
    )
    query_pos = jnp.tile(token_positions, GROUP)
    last_query = jnp.max(token_positions)
    scale = 1.0 / math.sqrt(HEAD_SIZE)
    start_state = (
        jnp.full((kv_heads, GROUP * tok_rows), -1e30, jnp.float32),
        jnp.zeros((kv_heads, GROUP * tok_rows), jnp.float32),
        jnp.zeros((kv_heads, GROUP * tok_rows, HEAD_SIZE), jnp.float32),
    )
    key_piece = lax.all_gather(rotated_keys, "seq", axis=0, tiled=True)
    value_piece = lax.all_gather(value_rows, "seq", axis=0, tiled=True)
    count = key_piece.shape[0]
    block = math.gcd(count, 1536)

    def visit(step, state):
        first = step * block
        key_block = lax.dynamic_slice_in_dim(key_piece, first, block, 0).reshape(
            block, kv_heads, HEAD_SIZE
        )
        value_block = lax.dynamic_slice_in_dim(value_piece, first, block, 0).reshape(
            block, kv_heads, HEAD_SIZE
        )
        row_ids = first + jnp.arange(block, dtype=jnp.int32)
        key_pos = span_lookup(span_order, row_ids // tok_rows) * tok_rows + row_ids % tok_rows

        def update(current):
            maxima, totals, sums = current
            scores = (
                jnp.einsum("kqd,nkd->kqn", grouped, key_block, preferred_element_type=jnp.float32)
                * scale
            )
            allowed = (key_pos[None, :] <= query_pos[:, None])[None, :, :]
            scores = jnp.where(allowed, scores, -1e30)
            fresh = jnp.maximum(maxima, jnp.max(scores, axis=2))
            weights = jnp.where(allowed, jnp.exp(scores - fresh[:, :, None]), 0.0)
            factor = jnp.exp(maxima - fresh)
            totals = totals * factor + jnp.sum(weights, axis=2)
            sums = sums * factor[:, :, None] + jnp.einsum(
                "kqn,nkd->kqd",
                weights.astype(jnp.bfloat16),
                value_block,
                preferred_element_type=jnp.float32,
            )
            return (fresh, totals, sums)

        return lax.cond(jnp.min(key_pos) <= last_query, update, lambda current: current, state)

    maxima, totals, sums = lax.fori_loop(0, count // block, visit, start_state)
    attended = (sums / totals[:, :, None]).astype(jnp.bfloat16)
    attended = (
        attended.reshape(kv_heads, GROUP, tok_rows, HEAD_SIZE)
        .transpose(2, 0, 1, 3)
        .reshape(tok_rows, query_heads * HEAD_SIZE)
    )
    partial_out = jnp.dot(
        attended,
        lax.all_gather(w_out, "seq", axis=1, tiled=True),
        preferred_element_type=jnp.float32,
    )
    mixed = lax.psum_scatter(
        partial_out.astype(jnp.bfloat16), "tp", scatter_dimension=1, tiled=True
    ).astype(jnp.float32)
    attn_out = mixed.astype(jnp.bfloat16)
    stream = local + mixed
    post_sq = lax.psum(jnp.sum(stream * stream, axis=1), "tp")
    normed = (
        stream
        * lax.rsqrt(post_sq / MODEL_WIDTH + eps)[:, None]
        * post_gain.astype(jnp.float32)[None, :]
    ).astype(jnp.bfloat16)
    return (attn_out, normed)


def solution(mesh):
    placed = (
        P("seq", "tp"),
        P(),
        P("tp"),
        P("seq", "tp"),
        P("tp"),
        P("seq", None, "tp"),
        P(None, "tp"),
        P("tp", "seq"),
        P("tp"),
    )
    return jax.shard_map(
        per_device,
        mesh=mesh,
        in_specs=placed,
        out_specs=(P("seq", "tp"), P("seq", "tp")),
        check_vma=False,
    )
```

profile of v0, /device:TPU:0, one launch (start us, length us, event | category | flops | bytes accessed | tf_op | source)
XLA Modules:
  0.0 499.7 jit_solution(17849845767442077635)
XLA Ops:
  7.9 1.9 copy.44
  9.9 5.5 %all-gather = bf16[4096]{0:T(1024)(128)(2,1)S(1)} all-gather(bf16[2048]{0:T(1024)(128)(2,1)} %param.15), channel_id=2, replica_groups=mesh['seq'=16,'tp'=2] {'tp'}, dimensions={0}, use_global_device_ids=true | all-gather | bytes 12288 | tf_op jit(solution)/shard_map/all_gather | solution.py:50
  16.1 17.4 %all-gather.9.cloned.1.call-done = bf16[128,4096]{1,0:T(8,128)(2,1)} async-done(((bf16[128,2048]{1,0:T(8,128)(2,1)}), bf16[128,4096]{1,0:T(8,128)(2,1)}) %all-gather.9.cloned.1.call-update) | async-done | bytes 1048592 | tf_op jit(solution)/shard_map/all_gather | solution.py:49
  35.1 75.6 %all-gather.11.cloned.1.call-done = bf16[4096,2,512]{2,0,1:T(8,128)(2,1)} async-done(((bf16[256,2,512]{2,0,1:T(8,128)(2,1)}), bf16[4096,2,512]{2,0,1:T(8,128)(2,1)}) %all-gather.11.cloned.1.call-update) | async-done | bytes 8388624 | tf_op jit(solution)/shard_map/all_gather | solution.py:67
  110.7 5.0 %convolution_add_fusion.1 = f32[128,2,512]{2,0,1:T(8,128)S(1)} fusion(bf16[4096,2,512]{2,0,1:T(8,128)(2,1)} %all-gather.11.cloned.1.call-done, bf16[128,4096]{1,0:T(8,128)(2,1)} %all-gather.9.cloned.1.call-done, f32[4096]{0:T(1024)S(1)} %mul.210, f32[128]{0:T(128)S(1)} %add_rsqrt_fusion.1, f32[2,512]{1,0:T(2,128)S(1)} %convert_element_type.69), kind=kOutput, calls=%fused_computation.39 | convolution fusion | flops 1075970048 | bytes 9982464 | tf_op jit(solution)/shard_map/tr,rkc->tkc/dot_general | solution.py:64
  121.5 35.1 %all-gather.19.cloned.1.call-done = bf16[2048,1,512]{2,0,1:T(8,128)(2,1)} async-done(((bf16[128,1,512]{2,0,1:T(8,128)(2,1)}), bf16[2048,1,512]{2,0,1:T(8,128)(2,1)}) %all-gather.19.cloned.1.call-update) | async-done | bytes 2097168 | tf_op jit(solution)/shard_map/all_gather | solution.py:96
  156.6 2.9 copy.48
  159.5 124.3 %all-gather.15.cloned.1.call-done = bf16[4096,2048]{1,0:T(8,128)(2,1)} async-done(((bf16[256,2048]{1,0:T(8,128)(2,1)}), bf16[4096,2048]{1,0:T(8,128)(2,1)}) %all-gather.15.cloned.1.call-update) | async-done | bytes 16777232 | tf_op jit(solution)/shard_map/all_gather | solution.py:60
  283.8 8.2 %fusion.21 = f32[16,8,16,128]{3,1,2,0:T(8,128)S(1)} fusion(bf16[4096,2048]{1,0:T(8,128)(2,1)} %all-gather.15.cloned.1.call-done, f32[2048]{0:T(1024)S(1)} %convert_element_type.72, bf16[128,4096]{1,0:T(8,128)(2,1)S(1)} %copy-done, f32[4096]{0:T(1024)S(1)} %mul.210, f32[128]{0:T(128)S(1)} %add_rsqrt_fusion.1), kind=kOutput, calls=%fused_computation.38 | convolution fusion | flops 2149842944 | bytes 18899456 | tf_op jit(solution)/shard_map/dot_general | solution.py:58
  293.3 32.3 %all-gather.13.cloned.1.call-done = bf16[2048,512]{0,1:T(8,128)(2,1)} async-done(((bf16[128,512]{0,1:T(8,128)(2,1)}), bf16[2048,512]{0,1:T(8,128)(2,1)}) %all-gather.13.cloned.1.call-update) | async-done | bytes 2097168 | tf_op jit(solution)/shard_map/all_gather | solution.py:95
  326.7 33.3 %while.20 = (s32[]{:T(128)}, f32[4,512]{1,0:T(4,128)S(1)}, f32[4,512]{1,0:T(4,128)S(1)}, f32[4,512,128]{2,1,0:T(8,128)}, s32[16]{0:T(128)S(1)}, /*index=5*/s32[]...) while((s32[]{:T(128)}, f32[4,512]{1,0:T(4,128)S(1)}, ...), condition=%wide.region_10.11_spmd.clone, body=%wide.region_3.10_spmd.clone.sunk | while | flops 551332864 | bytes 27935672 | solution.py:133
  328.7 6.3 %conditional.3 = ((f32[4,512]{1,0:T(4,128)S(1)}, f32[4,512]{1,0:T(4,128)S(1)}, f32[4,512,128]{2,1,0:T(8,128)})) conditional(s32[]{:T(128)} %convert_element_type.117, (f32[4,512]{1,0:T(4,128)S(1)}, f32[4,512]{1,0:T(4,128)S(1)}, f32[4,512,128]{2,1,0:T(8,128)}) %tuple.77, (s32[512]{0:T(512)S(1)}, s32[128]{0:T(128)S(1)}, s32[]{:T(128)}, ...), branch_computations={%region_6.6_spmd, %region_7.9_spmd} | conditional | flops 551292928 | bytes 27925118 | solution.py:131
  332.2 1.8 fusion.8
  337.0 6.3 %conditional.3 = ((f32[4,512]{1,0:T(4,128)S(1)}, f32[4,512]{1,0:T(4,128)S(1)}, f32[4,512,128]{2,1,0:T(8,128)})) conditional(s32[]{:T(128)} %convert_element_type.117, (f32[4,512]{1,0:T(4,128)S(1)}, f32[4,512]{1,0:T(4,128)S(1)}, f32[4,512,128]{2,1,0:T(8,128)}) %tuple.77, (s32[512]{0:T(512)S(1)}, s32[128]{0:T(128)S(1)}, s32[]{:T(128)}, ...), branch_computations={%region_6.6_spmd, %region_7.9_spmd} | conditional | flops 551292928 | bytes 27925118 | solution.py:131
  340.6 1.8 fusion.8
  345.4 6.3 %conditional.3 = ((f32[4,512]{1,0:T(4,128)S(1)}, f32[4,512]{1,0:T(4,128)S(1)}, f32[4,512,128]{2,1,0:T(8,128)})) conditional(s32[]{:T(128)} %convert_element_type.117, (f32[4,512]{1,0:T(4,128)S(1)}, f32[4,512]{1,0:T(4,128)S(1)}, f32[4,512,128]{2,1,0:T(8,128)}) %tuple.77, (s32[512]{0:T(512)S(1)}, s32[128]{0:T(128)S(1)}, s32[]{:T(128)}, ...), branch_computations={%region_6.6_spmd, %region_7.9_spmd} | conditional | flops 551292928 | bytes 27925118 | solution.py:131
  348.9 1.8 fusion.8
  353.7 6.3 %conditional.3 = ((f32[4,512]{1,0:T(4,128)S(1)}, f32[4,512]{1,0:T(4,128)S(1)}, f32[4,512,128]{2,1,0:T(8,128)})) conditional(s32[]{:T(128)} %convert_element_type.117, (f32[4,512]{1,0:T(4,128)S(1)}, f32[4,512]{1,0:T(4,128)S(1)}, f32[4,512,128]{2,1,0:T(8,128)}) %tuple.77, (s32[512]{0:T(512)S(1)}, s32[128]{0:T(128)S(1)}, s32[]{:T(128)}, ...), branch_computations={%region_6.6_spmd, %region_7.9_spmd} | conditional | flops 551292928 | bytes 27925118 | solution.py:131
  357.2 1.8 fusion.8
  361.8 94.8 %all-gather.17.cloned.1.call-done = bf16[2048,4096]{1,0:T(8,128)(2,1)} async-done(((bf16[2048,256]{1,0:T(8,128)(2,1)}), bf16[2048,4096]{1,0:T(8,128)(2,1)}) %all-gather.17.cloned.1.call-update) | async-done | bytes 16777232 | tf_op jit(solution)/shard_map/all_gather | solution.py:142
  456.6 9.2 %convolution_convert_fusion = bf16[128,4096]{1,0:T(8,128)(2,1)} fusion(bf16[128,2048]{0,1:T(8,128)(2,1)S(1)} %bitcast.47, bf16[2048,4096]{1,0:T(8,128)(2,1)} %all-gather.17.cloned.1.call-done), kind=kOutput, calls=%fused_computation.31 | convolution fusion | flops 2148007936 | bytes 18350080 | tf_op jit(solution)/shard_map/dot_general | solution.py:140
  465.9 18.7 %reduce-scatter.2.cloned.1.call-done = bf16[128,2048]{1,0:T(8,128)(2,1)} async-done(((bf16[128,4096]{1,0:T(8,128)(2,1)}), bf16[128,2048]{1,0:T(8,128)(2,1)}) %reduce-scatter.2.cloned.1.call-update) | async-done | bytes 524304 | tf_op jit(solution)/shard_map/reduce_scatter | solution.py:145
  485.9 4.9 psum.7
  490.8 2.0 multiply_convert_fusion
  (113 shorter events, 34.3 us)
Async XLA Ops:
  7.2 26.4 %all-gather.9.cloned.1.call-start = ((), (), s32[]{:S(2)}) async-start(), calls=%async_computation.1 | async-start | bytes 1572864 | tf_op jit(solution)/shard_map/all_gather | solution.py:49
  7.9 102.8 %all-gather.11.cloned.1.call-start = ((), (), s32[]{:S(2)}) async-start(), calls=%async_computation.2 | async-start | bytes 8912896 | tf_op jit(solution)/shard_map/all_gather | solution.py:67
  9.9 146.8 %all-gather.19.cloned.1.call-start = ((), (), s32[]{:S(2)}) async-start(), calls=%async_computation.7 | async-start | bytes 2228224 | tf_op jit(solution)/shard_map/all_gather | solution.py:96
  35.1 81.9 %copy-start.4 = (s32[16]{0:T(128)S(1)}, s32[16]{0:T(128)}, u32[]{:S(2)}) copy-start(s32[16]{0:T(128)} %param.14) | copy-start | bytes 196
  115.7 5.2 %copy-start.5 = (bf16[2048]{0:T(1024)(128)(2,1)S(1)}, bf16[2048]{0:T(1024)(128)(2,1)}, u32[]{:S(2)}) copy-start(bf16[2048]{0:T(1024)(128)(2,1)} %param.17) | copy-start | bytes 12292
  116.4 167.4 %all-gather.15.cloned.1.call-start = ((), (), s32[]{:S(2)}) async-start(), calls=%async_computation.4 | async-start | bytes 17825792 | tf_op jit(solution)/shard_map/all_gather | solution.py:60
  117.0 166.8 %copy-start = (bf16[128,4096]{1,0:T(8,128)(2,1)S(1)}, bf16[128,4096]{1,0:T(8,128)(2,1)}, u32[]{:S(2)}) copy-start(bf16[128,4096]{1,0:T(8,128)(2,1)} %all-gather.9.cloned.1.call-done) | copy-start | bytes 3145732
  117.0 208.7 %all-gather.13.cloned.1.call-start = ((), (), s32[]{:S(2)}) async-start(), calls=%async_computation.3 | async-start | bytes 2228224 | tf_op jit(solution)/shard_map/all_gather | solution.py:95
  120.1 336.6 %all-gather.17.cloned.1.call-start = ((), (), s32[]{:S(2)}) async-start(), calls=%async_computation.5 | async-start | bytes 17825792 | tf_op jit(solution)/shard_map/all_gather | solution.py:142
  120.7 363.9 %reduce-scatter.2.cloned.1.call-start = ((), (), s32[]{:S(2)}) async-start(), calls=%async_computation.6 | async-start | bytes 1572864 | tf_op jit(solution)/shard_map/reduce_scatter | solution.py:145
  330.1 2.1 copy-start.2
  334.0 1.0 copy-start.3
  338.4 2.1 copy-start.2
  342.4 1.0 copy-start.3
  346.8 2.1 copy-start.2
  350.7 1.0 copy-start.3
  355.1 2.1 copy-start.2
  359.0 1.0 copy-start.3
  456.6 9.2 %copy-start.6 = (bf16[2048]{0:T(1024)(128)(2,1)S(1)}, bf16[2048]{0:T(1024)(128)(2,1)}, u32[]{:S(2)}) copy-start(bf16[2048]{0:T(1024)(128)(2,1)} %param.21) | copy-start | bytes 12292
  456.6 27.9 %copy-start.1 = (bf16[128,2048]{1,0:T(8,128)(2,1)S(1)}, bf16[128,2048]{1,0:T(8,128)(2,1)}, u32[]{:S(2)}) copy-start(bf16[128,2048]{1,0:T(8,128)(2,1)} %param.13) | copy-start | bytes 1572868
Sparse Core Ops, SparseCore 0:
  9.5 23.9 all-gather.8
  36.3 74.2 all-gather.10
  116.5 40.0 all-gather.18
  158.6 125.1 all-gather.14
  286.4 39.2 all-gather.12
  327.7 128.9 all-gather.16
  466.0 18.5 reduce-scatter.1
where the time goes:
time: 500 us
  waiting for transfers between devices  400 us (80%)
  matrix products  33.6 us (7%)
  other arithmetic  18.1 us (4%)
  local copies, waits for them, and re-layouts  16.7 us (3%)
  between operations  15 us (3%)
  blocking collectives  10.4 us (2%)
  loops' own time  5.46 us (1%)
    all_gather x1, waiting for transfers between devices, per_device(): lax.all_gather(w_query, 'seq', axis=0, tiled=True)  124 us
    all_gather x1, waiting for transfers between devices, per_device(): lax.all_gather(w_out, 'seq', axis=1, tiled=True)  94.8 us
    all_gather x1, waiting for transfers between devices, per_device(): lax.all_gather(key_value_weight, 'seq', axis=0, tiled=True)  75.6 us
    all_gather x1, waiting for transfers between devices, per_device(): value_piece = lax.all_gather(value_rows, 'seq', axis=0, tiled=True)  35.1 us
    all_gather x1, waiting for transfers between devices, per_device(): key_piece = lax.all_gather(rotated_keys, 'seq', axis=0, tiled=True)  32.3 us
    reduce_scatter x1, waiting for transfers between devices, per_device(): lax.psum_scatter(partial_out.astype(jnp.bfloat16), 'tp', scatter_dimensio...  18.7 us
    all_gather x1, waiting for transfers between devices, per_device(): lax.all_gather(hidden_in, 'tp', axis=1, tiled=True)  17.4 us
  transfers between devices with their start and end apart: 7, of which 7 were waited for; matrix products, arithmetic and copies ran while one was open for 9% of the time, Pallas kernels for 0%

commit v1 on v0

--- a/solution.py
+++ b/solution.py
@@ -92,8 +92,13 @@
         jnp.zeros((kv_heads, GROUP * tok_rows), jnp.float32),
         jnp.zeros((kv_heads, GROUP * tok_rows, HEAD_SIZE), jnp.float32),
     )
-    key_piece = lax.all_gather(rotated_keys, "seq", axis=0, tiled=True)
-    value_piece = lax.all_gather(value_rows, "seq", axis=0, tiled=True)
+    key_piece, value_piece = jnp.split(
+        lax.all_gather(
+            jnp.concatenate([rotated_keys, value_rows], axis=1), "seq", axis=0, tiled=True
+        ),
+        [rotated_keys.shape[1]],
+        axis=1,
+    )
     count = key_piece.shape[0]
     block = math.gcd(count, 1536)
 

time: 500 us -> 467 us (0.934)
  waiting for transfers between devices: 400 us -> 358 us
  local copies, waits for them, and re-layouts: 16.7 us -> 23.9 us
    all_gather x2 -> x1, waiting for transfers between devices: 67.4 us -> 47 us  [per_device(): lax.all_gather(jnp.concatenate([rotated_keys, value_rows], axis=1), 'seq'...]
    all_gather x1, waiting for transfers between devices: 94.8 us -> 84.1 us  [per_device(): lax.all_gather(w_out, 'seq', axis=1, tiled=True)]
    all_gather x1, waiting for transfers between devices: 124 us -> 115 us  [per_device(): lax.all_gather(w_query, 'seq', axis=0, tiled=True)]
  transfers between devices with their start and end apart: 7 -> 6, of which waited for: 7 -> 6; matrix products, arithmetic and copies ran while one was open for 9% -> 12% of each run, Pallas kernels for 0% -> 0%
where the time goes in v1:
time: 467 us
  waiting for transfers between devices  358 us (77%)
  matrix products  33.6 us (7%)
  local copies, waits for them, and re-layouts  23.9 us (5%)
  other arithmetic  19.8 us (4%)
  between operations  14.9 us (3%)
  blocking collectives  10.4 us (2%)
  loops' own time  5.66 us (1%)
    all_gather x1, waiting for transfers between devices, per_device(): lax.all_gather(w_query, 'seq', axis=0, tiled=True)  115 us
    all_gather x1, waiting for transfers between devices, per_device(): lax.all_gather(w_out, 'seq', axis=1, tiled=True)  84.1 us
    all_gather x1, waiting for transfers between devices, per_device(): lax.all_gather(key_value_weight, 'seq', axis=0, tiled=True)  75.7 us
    all_gather x1, waiting for transfers between devices, per_device(): lax.all_gather(jnp.concatenate([rotated_keys, value_rows], axis=1), 'seq'...  47 us
    reduce_scatter x1, waiting for transfers between devices, per_device(): lax.psum_scatter(partial_out.astype(jnp.bfloat16), 'tp', scatter_dimensio...  18.7 us
    all_gather x1, waiting for transfers between devices, per_device(): lax.all_gather(hidden_in, 'tp', axis=1, tiled=True)  15.1 us
  transfers between devices with their start and end apart: 6, of which 6 were waited for; matrix products, arithmetic and copies ran while one was open for 12% of the time, Pallas kernels for 0%

profile of v1, /device:TPU:0, one launch (start us, length us, event | category | flops | bytes accessed | tf_op | source)
XLA Modules:
  0.0 466.6 jit_solution(11106249230774899603)
XLA Ops:
  7.9 1.9 copy.44
  9.9 5.5 %all-gather = bf16[4096]{0:T(1024)(128)(2,1)S(1)} all-gather(bf16[2048]{0:T(1024)(128)(2,1)} %param.15), channel_id=2, replica_groups=mesh['seq'=16,'tp'=2] {'tp'}, dimensions={0}, use_global_device_ids=true | all-gather | bytes 12288 | tf_op jit(solution)/shard_map/all_gather | solution.py:50
  18.4 15.1 %all-gather.7.cloned.1.call-done = bf16[128,4096]{1,0:T(8,128)(2,1)} async-done(((bf16[128,2048]{1,0:T(8,128)(2,1)}), bf16[128,4096]{1,0:T(8,128)(2,1)}) %all-gather.7.cloned.1.call-update) | async-done | bytes 1048592 | tf_op jit(solution)/shard_map/all_gather | solution.py:49
  35.1 75.7 %all-gather.9.cloned.1.call-done = bf16[4096,2,512]{2,0,1:T(8,128)(2,1)} async-done(((bf16[256,2,512]{2,0,1:T(8,128)(2,1)}), bf16[4096,2,512]{2,0,1:T(8,128)(2,1)}) %all-gather.9.cloned.1.call-update) | async-done | bytes 8388624 | tf_op jit(solution)/shard_map/all_gather | solution.py:67
  110.7 5.0 %convolution_add_fusion.1 = f32[128,2,512]{2,0,1:T(8,128)S(1)} fusion(bf16[4096,2,512]{2,0,1:T(8,128)(2,1)} %all-gather.9.cloned.1.call-done, bf16[128,4096]{1,0:T(8,128)(2,1)} %all-gather.7.cloned.1.call-done, f32[4096]{0:T(1024)S(1)} %mul.210, f32[128]{0:T(128)S(1)} %add_rsqrt_fusion.1, f32[2,512]{1,0:T(2,128)S(1)} %convert_element_type.69), kind=kOutput, calls=%fused_computation.39 | convolution fusion | flops 1075970048 | bytes 9982464 | tf_op jit(solution)/shard_map/tr,rkc->tkc/dot_general | solution.py:64
  119.3 47.0 %all-gather.11.cloned.1.call-done = bf16[2048,1024]{1,0:T(8,128)(2,1)} async-done(((bf16[128,1024]{1,0:T(8,128)(2,1)}), bf16[2048,1024]{1,0:T(8,128)(2,1)}) %all-gather.11.cloned.1.call-update) | async-done | bytes 4194320 | tf_op jit(solution)/shard_map/all_gather | solution.py:96
  166.3 4.4 fusion.31
  170.8 3.0 copy.47
  173.8 4.1 copy.48
  177.9 115.4 %all-gather.13.cloned.1.call-done = bf16[4096,2048]{1,0:T(8,128)(2,1)} async-done(((bf16[256,2048]{1,0:T(8,128)(2,1)}), bf16[4096,2048]{1,0:T(8,128)(2,1)}) %all-gather.13.cloned.1.call-update) | async-done | bytes 16777232 | tf_op jit(solution)/shard_map/all_gather | solution.py:60
  293.3 8.2 %fusion.21 = f32[16,8,16,128]{3,1,2,0:T(8,128)S(1)} fusion(bf16[4096,2048]{1,0:T(8,128)(2,1)} %all-gather.13.cloned.1.call-done, f32[2048]{0:T(1024)S(1)} %convert_element_type.73, bf16[128,4096]{1,0:T(8,128)(2,1)S(1)} %copy-done, f32[4096]{0:T(1024)S(1)} %mul.210, f32[128]{0:T(128)S(1)} %add_rsqrt_fusion.1), kind=kOutput, calls=%fused_computation.38 | convolution fusion | flops 2149842944 | bytes 18899456 | tf_op jit(solution)/shard_map/dot_general | solution.py:58
  303.9 33.7 %while.20 = (s32[]{:T(128)}, f32[4,512]{1,0:T(4,128)S(1)}, f32[4,512]{1,0:T(4,128)S(1)}, f32[4,512,128]{2,1,0:T(8,128)}, s32[16]{0:T(128)S(1)}, /*index=5*/s32[]...) while((s32[]{:T(128)}, f32[4,512]{1,0:T(4,128)S(1)}, ...), condition=%wide.region_10.11_spmd.clone, body=%wide.region_3.10_spmd.clone.sunk | while | flops 551332864 | bytes 27935672 | solution.py:138
  306.0 6.3 %conditional.3 = ((f32[4,512]{1,0:T(4,128)S(1)}, f32[4,512]{1,0:T(4,128)S(1)}, f32[4,512,128]{2,1,0:T(8,128)})) conditional(s32[]{:T(128)} %convert_element_type.117, (f32[4,512]{1,0:T(4,128)S(1)}, f32[4,512]{1,0:T(4,128)S(1)}, f32[4,512,128]{2,1,0:T(8,128)}) %tuple.78, (s32[512]{0:T(512)S(1)}, s32[128]{0:T(128)S(1)}, s32[]{:T(128)}, ...), branch_computations={%region_6.6_spmd, %region_7.9_spmd} | conditional | flops 551292928 | bytes 27925118 | solution.py:136
  309.6 1.8 fusion.8
  314.4 6.3 %conditional.3 = ((f32[4,512]{1,0:T(4,128)S(1)}, f32[4,512]{1,0:T(4,128)S(1)}, f32[4,512,128]{2,1,0:T(8,128)})) conditional(s32[]{:T(128)} %convert_element_type.117, (f32[4,512]{1,0:T(4,128)S(1)}, f32[4,512]{1,0:T(4,128)S(1)}, f32[4,512,128]{2,1,0:T(8,128)}) %tuple.78, (s32[512]{0:T(512)S(1)}, s32[128]{0:T(128)S(1)}, s32[]{:T(128)}, ...), branch_computations={%region_6.6_spmd, %region_7.9_spmd} | conditional | flops 551292928 | bytes 27925118 | solution.py:136
  318.0 1.8 fusion.8
  322.9 6.3 %conditional.3 = ((f32[4,512]{1,0:T(4,128)S(1)}, f32[4,512]{1,0:T(4,128)S(1)}, f32[4,512,128]{2,1,0:T(8,128)})) conditional(s32[]{:T(128)} %convert_element_type.117, (f32[4,512]{1,0:T(4,128)S(1)}, f32[4,512]{1,0:T(4,128)S(1)}, f32[4,512,128]{2,1,0:T(8,128)}) %tuple.78, (s32[512]{0:T(512)S(1)}, s32[128]{0:T(128)S(1)}, s32[]{:T(128)}, ...), branch_computations={%region_6.6_spmd, %region_7.9_spmd} | conditional | flops 551292928 | bytes 27925118 | solution.py:136
  326.4 1.8 fusion.8
  331.3 6.3 %conditional.3 = ((f32[4,512]{1,0:T(4,128)S(1)}, f32[4,512]{1,0:T(4,128)S(1)}, f32[4,512,128]{2,1,0:T(8,128)})) conditional(s32[]{:T(128)} %convert_element_type.117, (f32[4,512]{1,0:T(4,128)S(1)}, f32[4,512]{1,0:T(4,128)S(1)}, f32[4,512,128]{2,1,0:T(8,128)}) %tuple.78, (s32[512]{0:T(512)S(1)}, s32[128]{0:T(128)S(1)}, s32[]{:T(128)}, ...), branch_computations={%region_6.6_spmd, %region_7.9_spmd} | conditional | flops 551292928 | bytes 27925118 | solution.py:136
  339.4 84.1 %all-gather.15.cloned.1.call-done = bf16[2048,4096]{1,0:T(8,128)(2,1)} async-done(((bf16[2048,256]{1,0:T(8,128)(2,1)}), bf16[2048,4096]{1,0:T(8,128)(2,1)}) %all-gather.15.cloned.1.call-update) | async-done | bytes 16777232 | tf_op jit(solution)/shard_map/all_gather | solution.py:147
  423.5 9.2 %convolution_convert_fusion = bf16[128,4096]{1,0:T(8,128)(2,1)} fusion(bf16[128,2048]{0,1:T(8,128)(2,1)S(1)} %bitcast.51, bf16[2048,4096]{1,0:T(8,128)(2,1)} %all-gather.15.cloned.1.call-done), kind=kOutput, calls=%fused_computation.31 | convolution fusion | flops 2148007936 | bytes 18350080 | tf_op jit(solution)/shard_map/dot_general | solution.py:145
  432.8 18.7 %reduce-scatter.2.cloned.1.call-done = bf16[128,2048]{1,0:T(8,128)(2,1)} async-done(((bf16[128,4096]{1,0:T(8,128)(2,1)}), bf16[128,2048]{1,0:T(8,128)(2,1)}) %reduce-scatter.2.cloned.1.call-update) | async-done | bytes 524304 | tf_op jit(solution)/shard_map/reduce_scatter | solution.py:150
  452.7 4.9 %psum.7 = f32[128]{0:T(128)S(1)} all-reduce(f32[128]{0:T(128)S(1)} %multiply_reduce_fusion), channel_id=1, replica_groups=mesh['seq'=16,'tp'=2] {'tp'}, use_global_device_ids=true, to_apply=%region_13.14 | all-reduce | flops 128 | bytes 1024 | tf_op jit(solution)/shard_map/psum | solution.py:155
  457.7 2.0 multiply_convert_fusion
  (113 shorter events, 36.2 us)
Async XLA Ops:
  7.2 26.4 %all-gather.7.cloned.1.call-start = ((), (), s32[]{:S(2)}) async-start(), calls=%async_computation.1 | async-start | bytes 1572864 | tf_op jit(solution)/shard_map/all_gather | solution.py:49
  7.9 102.8 %all-gather.9.cloned.1.call-start = ((), (), s32[]{:S(2)}) async-start(), calls=%async_computation.2 | async-start | bytes 8912896 | tf_op jit(solution)/shard_map/all_gather | solution.py:67
  9.9 156.5 %all-gather.11.cloned.1.call-start = ((), (), s32[]{:S(2)}) async-start(), calls=%async_computation.3 | async-start | bytes 4456448 | tf_op jit(solution)/shard_map/all_gather | solution.py:96
  115.8 3.5 copy-start.5
  117.2 176.1 %all-gather.13.cloned.1.call-start = ((), (), s32[]{:S(2)}) async-start(), calls=%async_computation.4 | async-start | bytes 17825792 | tf_op jit(solution)/shard_map/all_gather | solution.py:60
  117.8 305.7 %all-gather.15.cloned.1.call-start = ((), (), s32[]{:S(2)}) async-start(), calls=%async_computation.5 | async-start | bytes 17825792 | tf_op jit(solution)/shard_map/all_gather | solution.py:147
  118.4 333.1 %reduce-scatter.2.cloned.1.call-start = ((), (), s32[]{:S(2)}) async-start(), calls=%async_computation.6 | async-start | bytes 1572864 | tf_op jit(solution)/shard_map/reduce_scatter | solution.py:150
  170.8 122.6 %copy-start = (bf16[128,4096]{1,0:T(8,128)(2,1)S(1)}, bf16[128,4096]{1,0:T(8,128)(2,1)}, u32[]{:S(2)}) copy-start(bf16[128,4096]{1,0:T(8,128)(2,1)} %all-gather.7.cloned.1.call-done) | copy-start | bytes 3145732
  301.7 2.2 copy-start.4
  307.4 2.1 copy-start.2
  311.3 1.0 copy-start.3
  315.8 2.1 copy-start.2
  319.8 1.0 copy-start.3
  324.2 2.1 copy-start.2
  328.2 1.0 copy-start.3
  332.7 2.1 copy-start.2
  336.6 1.0 copy-start.3
  423.5 9.2 %copy-start.6 = (bf16[2048]{0:T(1024)(128)(2,1)S(1)}, bf16[2048]{0:T(1024)(128)(2,1)}, u32[]{:S(2)}) copy-start(bf16[2048]{0:T(1024)(128)(2,1)} %param.21) | copy-start | bytes 12292
  423.5 27.9 %copy-start.1 = (bf16[128,2048]{1,0:T(8,128)(2,1)S(1)}, bf16[128,2048]{1,0:T(8,128)(2,1)}, u32[]{:S(2)}) copy-start(bf16[128,2048]{1,0:T(8,128)(2,1)} %param.13) | copy-start | bytes 1572868
Sparse Core Ops, SparseCore 0:
  9.5 23.9 all-gather.6
  36.3 74.3 all-gather.8
  117.3 48.9 all-gather.10
  168.3 124.9 all-gather.12
  295.3 128.1 all-gather.14
  432.9 18.5 reduce-scatter.1
